TPU v7x, 32 devices: a whole 2x2x4 slice. The times are simulated.
32 devices in a mesh: clump: 8 (over z, y), grp: 4 (over x, core).
Axes of the slice: x: 2, y: 2, z: 4, core: 2. Of those that a mesh axis runs over, the one named last changes fastest.
Arguments:
- flux: float32 [32, 1024, 64], P(('clump', 'grp')), may hold values from -6 to 6
- patch_pft: int32 [32, 1024], P(('clump', 'grp')), may hold values from 0 to 15
- patch_wt: float32 [32, 1024], P(('clump', 'grp')), may hold values from 0.2 to 2
- patch_col: int32 [32, 1024], P(('clump', 'grp')), may hold values from 0 to 511, never falling along the last dimension, each value on 1 to 4 neighbouring positions
- col_wt: float32 [32, 512], P(('clump', 'grp')), may hold values from 0.2 to 2
- col_lu: int32 [32, 512], P(('clump', 'grp')), may hold values from 0 to 255, never falling along the last dimension, each value on 1 to 4 neighbouring positions
- lu_wt: float32 [32, 256], P(('clump', 'grp')), may hold values from 0.2 to 2
- lu_grid: int32 [32, 256], P(('clump', 'grp')), may hold values from 0 to 127, never falling along the last dimension, each value on 1 to 4 neighbouring positions
- cell_target: int32 [32, 128], P(('clump', 'grp')), may hold values from 0 to 4095, as said below
- patch_count: int32 [32], P(('clump', 'grp')), may hold values from 64 to 1024
- pft_scale: float32 [16, 64], replicated, may hold values from 0.3 to 3
- cpl_frac: float32 [4096], P(('clump', 'grp')), may hold values from 0.2 to 0.9
- cpl_field: float32 [4096, 64], P(('clump', 'grp')), may hold values from -6 to 6
Outputs:
- grid_merged: float32 [4096, 64], P(('clump', 'grp'))
- anomaly: float32 [32, 1024, 64], P(('clump', 'grp'))
Inputs may be any that keep to these rules, and one draw needn't show every extreme that they name: `patch_col`: within each device's row the column numbers never fall, and each column holds 1 to 4 patch slots. `col_lu`: within each device's row the landunit numbers never fall, and each landunit holds 1 to 4 columns. `lu_grid`: within each device's row the gridcell numbers never fall, and each gridcell holds 1 to 4 landunits. `cell_target`: all devices' entries together are a permutation of 0 to 4095; the coupler owner of an entry q is q // 128, and each device's 128 gridcells go to 16 owners, exactly 8 to each.
All inputs are finite; a program needn't handle non-finite values.
Results may differ from a plain program's by a relative error of at most 0.0003.
Values sent between devices are 32-bit elements; how exact they have to be, the bound alone decides.
A program may use at most 64 MiB of HBM per device.

v0:
```python
import jax
import jax.numpy as jnp
from jax import lax
from jax.sharding import PartitionSpec as P

HIGH = lax.Precision.HIGHEST


def window_pick(padded, start, relative, width):
    window = lax.dynamic_slice_in_dim(padded, start, width, 0)
    onehot = (relative[:, None] == jnp.arange(width, dtype=jnp.int32)[None, :]).astype(jnp.float32)
    return jnp.dot(onehot, window, precision=HIGH)


def per_device(
    flux,
    patch_pft,
    patch_wt,
    patch_col,
    col_wt,
    col_lu,
    lu_wt,
    lu_grid,
    cell_target,
    patch_count,
    pft_scale,
    cpl_frac,
    cpl_field,
):
    n_clump = lax.axis_size("clump")
    n_group = lax.axis_size("grp")
    n_devices = n_clump * n_group
    values = flux[0]
    patches = values.shape[0]
    width_vars = values.shape[1]
    cell_count = cell_target.shape[1]
    capacity = max(2, 2 * cell_count // n_devices)
    slot_total = n_devices * capacity
    block = min(512, patches)
    blocks = patches // block
    position = jnp.arange(patches, dtype=jnp.int32)
    alive_mask = (position < patch_count[0]).astype(jnp.float32)
    type_onehot = (
        patch_pft[0][:, None] == jnp.arange(pft_scale.shape[0], dtype=jnp.int32)[None, :]
    ).astype(jnp.float32)
    scaled = values * jnp.dot(type_onehot, pft_scale, precision=HIGH)
    col_table = jnp.stack([col_wt[0], col_lu[0].astype(jnp.float32)], axis=1)
    col_table = jnp.concatenate([col_table, jnp.zeros((block, 2), jnp.float32)], axis=0)
    lu_table = jnp.stack([lu_wt[0], lu_grid[0].astype(jnp.float32)], axis=1)
    lu_table = jnp.concatenate([lu_table, jnp.zeros((block, 2), jnp.float32)], axis=0)
    within = jnp.arange(block, dtype=jnp.int32)

    def gather_block(carry, entries):
        num_acc, den_acc = carry
        cols_blk, alive_blk, pwt_blk, scaled_blk = entries
        col_start = cols_blk[0]
        col_vals = window_pick(col_table, col_start, cols_blk - col_start, block)
        land_blk = col_vals[:, 1].astype(jnp.int32)
        land_start = land_blk[0]
        lu_vals = window_pick(lu_table, land_start, land_blk - land_start, block)
        home_blk = lu_vals[:, 1].astype(jnp.int32)
        weight_blk = alive_blk * pwt_blk * col_vals[:, 0] * lu_vals[:, 0]
        home_start = home_blk[0]
        cell_onehot = (within[:, None] == (home_blk - home_start)[None, :]).astype(jnp.float32)
        part_num = jnp.dot(cell_onehot, scaled_blk * weight_blk[:, None], precision=HIGH)
        part_den = jnp.dot(cell_onehot, weight_blk, precision=HIGH)
        old_num = lax.dynamic_slice_in_dim(num_acc, home_start, block, 0)
        old_den = lax.dynamic_slice_in_dim(den_acc, home_start, block, 0)
        num_acc = lax.dynamic_update_slice_in_dim(num_acc, old_num + part_num, home_start, 0)
        den_acc = lax.dynamic_update_slice_in_dim(den_acc, old_den + part_den, home_start, 0)
        return ((num_acc, den_acc), home_blk)

    start_acc = (
        jnp.zeros((cell_count + block, width_vars), jnp.float32),
        jnp.zeros((cell_count + block,), jnp.float32),
    )
    block_inputs = (
        patch_col[0].reshape(blocks, block),
        alive_mask.reshape(blocks, block),
        patch_wt[0].reshape(blocks, block),
        scaled.reshape(blocks, block, width_vars),
    )
    (num_acc, den_acc), home_blocks = lax.scan(gather_block, start_acc, block_inputs)
    cell_num = num_acc[:cell_count]
    cell_den = den_acc[:cell_count]
    target = cell_target[0]
    owner_dev = target // cell_count
    local_slot = target - owner_dev * cell_count
    same_owner = (owner_dev[:, None] == owner_dev[None, :]).astype(jnp.int32)
    earlier = (
        jnp.arange(cell_count, dtype=jnp.int32)[None, :]
        < jnp.arange(cell_count, dtype=jnp.int32)[:, None]
    ).astype(jnp.int32)
    rank_within = jnp.sum(same_owner * earlier, axis=1)
    slot = owner_dev * capacity + rank_within
    slot_onehot = (jnp.arange(slot_total, dtype=jnp.int32)[:, None] == slot[None, :]).astype(
        jnp.float32
    )
    slot_used = jnp.sum(slot_onehot, axis=1)
    send_slot = jnp.dot(slot_onehot, local_slot.astype(jnp.float32), precision=HIGH) + (
        1.0 - slot_used
    ) * float(cell_count)
    send_slot = send_slot.reshape(n_clump, n_group, capacity)
    cell_mean = cell_num / jnp.maximum(cell_den, 1.0)[:, None]
    send_mean = jnp.dot(slot_onehot, cell_mean, precision=HIGH)
    outgoing = (send_mean.reshape(n_clump, n_group, capacity, width_vars), send_slot)
    incoming = (
        lax.all_to_all(
            lax.all_to_all(outgoing[0], "clump", split_axis=0, concat_axis=0, tiled=True),
            "grp",
            split_axis=1,
            concat_axis=1,
            tiled=True,
        ),
        lax.all_to_all(
            lax.all_to_all(outgoing[1], "clump", split_axis=0, concat_axis=0, tiled=True),
            "grp",
            split_axis=1,
            concat_axis=1,
            tiled=True,
        ),
    )
    slot_ids = incoming[-1].reshape(-1).astype(jnp.int32)
    owner_onehot = (slot_ids[:, None] == jnp.arange(cell_count, dtype=jnp.int32)[None, :]).astype(
        jnp.float32
    )
    owned_mean = jnp.dot(owner_onehot.T, incoming[0].reshape(-1, width_vars), precision=HIGH)
    grid_merged = cpl_frac[:, None] * owned_mean + (1.0 - cpl_frac)[:, None] * cpl_field
    reply_rows = jnp.dot(owner_onehot, grid_merged, precision=HIGH).reshape(
        n_clump, n_group, capacity, width_vars
    )
    returned = lax.all_to_all(
        lax.all_to_all(reply_rows, "clump", split_axis=0, concat_axis=0, tiled=True),
        "grp",
        split_axis=1,
        concat_axis=1,
        tiled=True,
    )
    cell_merged = jnp.dot(slot_onehot.T, returned.reshape(slot_total, width_vars), precision=HIGH)
    merged_table = jnp.concatenate(
        [cell_merged, jnp.zeros((block, width_vars), jnp.float32)], axis=0
    )

    def spread_block(entries):
        home_blk, alive_blk, scaled_blk = entries
        home_start = home_blk[0]
        picked = window_pick(merged_table, home_start, home_blk - home_start, block)
        return alive_blk[:, None] * (scaled_blk - picked)

    anomaly = lax.map(
        spread_block,
        (home_blocks, alive_mask.reshape(blocks, block), scaled.reshape(blocks, block, width_vars)),
    )
    return (grid_merged, anomaly.reshape(1, patches, width_vars))


def solution(mesh):
    return jax.shard_map(
        per_device,
        mesh=mesh,
        in_specs=(
            P(("clump", "grp"), None, None),
            P(("clump", "grp"), None),
            P(("clump", "grp"), None),
            P(("clump", "grp"), None),
            P(("clump", "grp"), None),
            P(("clump", "grp"), None),
            P(("clump", "grp"), None),
            P(("clump", "grp"), None),
            P(("clump", "grp"), None),
            P(("clump", "grp")),
            P(),
            P(("clump", "grp")),
            P(("clump", "grp"), None),
        ),
        out_specs=(P(("clump", "grp"), None), P(("clump", "grp"), None, None)),
        check_vma=False,
    )
```

profile of v0, /device:TPU:0, one launch (start us, length us, event | category | flops | bytes accessed | tf_op | source)
XLA Modules:
  0.0 106.9 jit_solution(788008277498538944)
XLA Ops:
  2.6 7.4 %all-to-all-start = ((f32[8,4,8]{2,1,0:T(4,128)}), f32[8,4,8]{2,1,0:T(4,128)S(1)}, u32[]{:S(2)}, u32[]{:S(2)}) async-start(f32[8,4,8]{2,1,0:T(4,128)} %reshape.154), calls=%async_computation | async-start | bytes 32768 | tf_op jit(solution)/shard_map/all_to_all | solution.py:116
  10.1 1.5 %convolution_multiply_fusion = f32[1024,64]{0,1:T(8,128)S(1)} fusion(f32[16,64]{1,0:T(8,128)S(1)} %copy-done, f32[1,1024,64]{1,2,0:T(8,128)} %param.17, s32[1024]{0:T(1024)S(1)} %bitcast.148), kind=kOutput, calls=%fused_computation.43 | convolution fusion | flops 12664832 | bytes 532480 | tf_op jit(solution)/shard_map/dot_general | solution.py:46
  17.9 26.6 %while.26 = (s32[]{:T(128)}, f32[640,64]{0,1:T(8,128)S(1)}, f32[640]{0:T(1024)S(1)}, s32[2,512]{1,0:T(2,128)S(1)}, s32[2,512]{1,0:T(2,128)S(1)}, /*index=5*/f32[...) while((s32[]{:T(128)}, f32[640,64]{0,1:T(8,128)S(1)}, ...), condition=%wide.region_3.4_spmd.clone, body=%wide.region_2.3_spmd.clone.sunk | while | flops 218176016 | bytes 1268031 | solution.py:83
  29.6 0.8 dynamic_update_slice.24
  42.8 1.0 dynamic_update_slice.24
  44.8 0.8 reshape.183
  45.6 6.0 %all-to-all-start.2 = ((f32[8,1,2048]{2,1,0:T(1,128)}), f32[8,1,2048]{2,1,0:T(1,128)S(1)}, u32[]{:S(2)}, u32[]{:S(2)}) async-start(f32[8,1,2048]{2,1,0:T(1,128)} %reshape.183), calls=%async_computation.2 | async-start | bytes 131072 | tf_op jit(solution)/shard_map/all_to_all | solution.py:109
  52.2 6.3 %all-to-all-done.2 = f32[8,1,2048]{2,1,0:T(1,128)S(1)} async-done(((f32[8,1,2048]{2,1,0:T(1,128)}), f32[8,1,2048]{2,1,0:T(1,128)S(1)}, u32[]{:S(2)}, u32[]{:S(2)}) %all-to-all-start.2) | async-done | bytes 65568 | tf_op jit(solution)/shard_map/all_to_all | solution.py:109
  58.5 3.3 %all-to-all-start.1 = ((f32[8,4,8]{2,0,1:T(8,128)}), f32[8,4,8]{2,0,1:T(8,128)S(1)}, u32[]{:S(2)}, u32[]{:S(2)}) async-start(f32[8,4,8]{2,0,1:T(8,128)} %copy.47), calls=%async_computation.1 | async-start | bytes 32768 | tf_op jit(solution)/shard_map/all_to_all | solution.py:115
  62.3 0.8 reduce.8
  63.2 0.8 reshape.185
  64.0 1.6 %all-to-all-done.1 = f32[8,4,8]{2,0,1:T(8,128)S(1)} async-done(((f32[8,4,8]{2,0,1:T(8,128)}), f32[8,4,8]{2,0,1:T(8,128)S(1)}, u32[]{:S(2)}, u32[]{:S(2)}) %all-to-all-start.1) | async-done | bytes 1056 | tf_op jit(solution)/shard_map/all_to_all | solution.py:115
  65.6 3.3 %all-to-all-start.3 = ((f32[4,1,4096]{2,1,0:T(1,128)}), f32[4,1,4096]{2,1,0:T(1,128)S(1)}, u32[]{:S(2)}, u32[]{:S(2)}) async-start(f32[4,1,4096]{2,1,0:T(1,128)} %reshape.185), calls=%async_computation.3 | async-start | bytes 131072 | tf_op jit(solution)/shard_map/all_to_all | solution.py:108
  69.0 3.9 %all-to-all-done.3 = f32[4,1,4096]{2,1,0:T(1,128)S(1)} async-done(((f32[4,1,4096]{2,1,0:T(1,128)}), f32[4,1,4096]{2,1,0:T(1,128)S(1)}, u32[]{:S(2)}, u32[]{:S(2)}) %all-to-all-start.3) | async-done | bytes 65568 | tf_op jit(solution)/shard_map/all_to_all | solution.py:108
  72.9 0.8 reduce.9
  75.7 9.3 %all_to_all.30 = f32[8,1,2048]{2,1,0:T(1,128)S(1)} all-to-all(f32[8,1,2048]{2,1,0:T(1,128)S(1)} %reshape.187), channel_id=1, replica_groups=mesh['clump'=8,'grp'=4] {'clump'}, dimensions={0} | all-to-all | bytes 131072 | tf_op jit(solution)/shard_map/all_to_all | solution.py:133
  85.0 0.8 reduce.10
  86.6 3.3 %all-to-all-start.5 = ((f32[4,1,4096]{2,1,0:T(1,128)}), f32[4,1,4096]{2,1,0:T(1,128)S(1)}, u32[]{:S(2)}, u32[]{:S(2)}) async-start(f32[4,1,4096]{2,1,0:T(1,128)} %reshape.189), calls=%async_computation.5 | async-start | bytes 131072 | tf_op jit(solution)/shard_map/all_to_all | solution.py:132
  89.9 4.1 %all-to-all-done.5 = f32[4,1,4096]{2,1,0:T(1,128)S(1)} async-done(((f32[4,1,4096]{2,1,0:T(1,128)}), f32[4,1,4096]{2,1,0:T(1,128)S(1)}, u32[]{:S(2)}, u32[]{:S(2)}) %all-to-all-start.5) | async-done | bytes 65568 | tf_op jit(solution)/shard_map/all_to_all | solution.py:132
  94.0 0.8 reduce.11
  95.3 10.7 %while.25 = (s32[]{:T(128)}, f32[2,512,64]{1,0,2:T(2,128)S(1)}, f32[2,512]{1,0:T(2,128)S(1)}, f32[2,512,64]{1,0,2:T(2,128)S(1)}, s32[2,512]{1,0:T(2,128)S(1)}, /...) while((s32[]{:T(128)}, f32[2,512,64]{1,0,2:T(2,128)S(1)}, f32[2,512]{1,0:T(2,128)S(1)}, ...), condition=%wide.region_5.6_spmd, body=%wide.region_4.5_spmd.sunk | while | flops 201654784 | bytes 1192099 | solution.py:150
  99.4 1.2 %dynamic_update_slice.22 = f32[2,512,64]{1,0,2:T(2,128)S(1)} dynamic-update-slice(f32[2,512,64]{1,0,2:T(2,128)S(1)} %get-tuple-element.402, f32[1,512,64]{1,0,2:T(1,128)S(1)} %copy.81, s32[]{:T(128)} %get-tuple-element.401, s32[]{:T(128)} %constant.46.clone.1..sunk, s32[]{:T(128)} %constant.46.clone.1..sunk) | dynamic-update-slice | bytes 262148 | tf_op jit(solution)/shard_map/while/body/jit(dynamic_update_index_in_dim)/dynamic_update_slice | solution.py:150
  104.8 1.2 %dynamic_update_slice.22 = f32[2,512,64]{1,0,2:T(2,128)S(1)} dynamic-update-slice(f32[2,512,64]{1,0,2:T(2,128)S(1)} %get-tuple-element.402, f32[1,512,64]{1,0,2:T(1,128)S(1)} %copy.81, s32[]{:T(128)} %get-tuple-element.401, s32[]{:T(128)} %constant.46.clone.1..sunk, s32[]{:T(128)} %constant.46.clone.1..sunk) | dynamic-update-slice | bytes 262148 | tf_op jit(solution)/shard_map/while/body/jit(dynamic_update_index_in_dim)/dynamic_update_slice | solution.py:150
  106.0 0.9 reshape.160
  (117 shorter events, 29.9 us)
Async XLA Ops:
  0.6 9.4 %copy-start = (f32[16,64]{1,0:T(8,128)S(1)}, f32[16,64]{1,0:T(8,128)}, u32[]{:S(2)}) copy-start(f32[16,64]{1,0:T(8,128)} %param.27) | copy-start | bytes 12292
  0.6 0.7 copy-start.11
  2.6 7.5 %copy-start.3 = (s32[1,1024]{1,0:T(1,128)S(1)}, s32[1,1024]{1,0:T(1,128)}, u32[]{:S(2)}) copy-start(s32[1,1024]{1,0:T(1,128)} %param.18) | copy-start | bytes 12292
  2.6 42.9 %all-to-all-start = ((f32[8,4,8]{2,1,0:T(4,128)}), f32[8,4,8]{2,1,0:T(4,128)S(1)}, u32[]{:S(2)}, u32[]{:S(2)}) async-start(f32[8,4,8]{2,1,0:T(4,128)} %reshape.154), calls=%async_computation | async-start | bytes 32768 | tf_op jit(solution)/shard_map/all_to_all | solution.py:116
  12.5 0.7 copy-start.6
  13.2 0.7 copy-start.4
  14.5 0.7 copy-start.5
  15.9 0.7 copy-start.8
  16.5 0.7 copy-start.7
  17.2 0.7 copy-start.9
  45.6 12.9 %all-to-all-start.2 = ((f32[8,1,2048]{2,1,0:T(1,128)}), f32[8,1,2048]{2,1,0:T(1,128)S(1)}, u32[]{:S(2)}, u32[]{:S(2)}) async-start(f32[8,1,2048]{2,1,0:T(1,128)} %reshape.183), calls=%async_computation.2 | async-start | bytes 131072 | tf_op jit(solution)/shard_map/all_to_all | solution.py:109
  58.5 7.1 %all-to-all-start.1 = ((f32[8,4,8]{2,0,1:T(8,128)}), f32[8,4,8]{2,0,1:T(8,128)S(1)}, u32[]{:S(2)}, u32[]{:S(2)}) async-start(f32[8,4,8]{2,0,1:T(8,128)} %copy.47), calls=%async_computation.1 | async-start | bytes 32768 | tf_op jit(solution)/shard_map/all_to_all | solution.py:115
  64.0 4.9 %copy-start.10 = (f32[128]{0:T(128)S(1)}, f32[128]{0:T(128)}, u32[]{:S(2)}) copy-start(f32[128]{0:T(128)} %param.28) | copy-start | bytes 1540
  65.6 7.4 %all-to-all-start.3 = ((f32[4,1,4096]{2,1,0:T(1,128)}), f32[4,1,4096]{2,1,0:T(1,128)S(1)}, u32[]{:S(2)}, u32[]{:S(2)}) async-start(f32[4,1,4096]{2,1,0:T(1,128)} %reshape.185), calls=%async_computation.3 | async-start | bytes 131072 | tf_op jit(solution)/shard_map/all_to_all | solution.py:108
  73.9 0.8 copy-start.2
  75.0 0.6 copy-start.1
  86.6 7.4 %all-to-all-start.5 = ((f32[4,1,4096]{2,1,0:T(1,128)}), f32[4,1,4096]{2,1,0:T(1,128)S(1)}, u32[]{:S(2)}, u32[]{:S(2)}) async-start(f32[4,1,4096]{2,1,0:T(1,128)} %reshape.189), calls=%async_computation.5 | async-start | bytes 131072 | tf_op jit(solution)/shard_map/all_to_all | solution.py:132
where the time goes:
time: 108 us; the launch traced here: 107 us
  starting transfers between devices  23.3 us (22%)
  local copies, waits for them, and re-layouts  20.7 us (19%)
  waiting for transfers between devices  15.9 us (15%)
  loops' own time  15.6 us (14%)
  other arithmetic  11.2 us (10%)
  blocking collectives  9.29 us (9%)
  matrix products  9.28 us (9%)
  between operations  1.59 us (1%)
    another operation x1, loops' own time, per_device(): lax.scan(gather_block, start_acc, block_inputs)  11.6 us
    all_to_all x1, blocking collectives, per_device(): lax.all_to_all(reply_rows, 'clump', split_axis=0, concat_axis=0, tiled=True)  9.29 us
    unnamed x34, local copies, waits for them, and re-layouts  7.96 us
    all_to_all x1, starting transfers between devices, per_device(): lax.all_to_all(outgoing[1], 'clump', split_axis=0, concat_axis=0, tiled=T...  7.44 us
    all_to_all x1, waiting for transfers between devices, per_device(): lax.all_to_all(outgoing[0], 'clump', split_axis=0, concat_axis=0, tiled=T...  6.3 us
    all_to_all x1, starting transfers between devices, per_device(): lax.all_to_all(outgoing[0], 'clump', split_axis=0, concat_axis=0, tiled=T...  5.99 us
    all_to_all x1, waiting for transfers between devices, per_device(): lax.all_to_all(lax.all_to_all(reply_rows, 'clump', split_axis=0, concat_a...  4.08 us
    another operation x1, loops' own time, per_device(): lax.map(spread_block, (home_blocks, alive_mask.reshape(blocks, block), sc...  3.99 us
  transfers between devices with their start and end apart: 5, of which 4 were waited for; matrix products, arithmetic and copies ran while one was open for 22% of the time, Pallas kernels for 0%

commit v1 on v0

--- a/solution.py
+++ b/solution.py
@@ -112,12 +112,22 @@
             concat_axis=1,
             tiled=True,
         ),
-        lax.all_to_all(
-            lax.all_to_all(outgoing[1], "clump", split_axis=0, concat_axis=0, tiled=True),
-            "grp",
-            split_axis=1,
-            concat_axis=1,
-            tiled=True,
+        jnp.concatenate(
+            lax.all_to_all(
+                jnp.stack(
+                    jnp.split(
+                        lax.all_to_all(
+                            outgoing[1], "clump", split_axis=0, concat_axis=0, tiled=True
+                        ),
+                        lax.axis_size("grp"),
+                        axis=1,
+                    )
+                ),
+                "grp",
+                0,
+                0,
+            ),
+            axis=1,
         ),
     )
     slot_ids = incoming[-1].reshape(-1).astype(jnp.int32)

time: 108 us -> 108 us (level)
  no operation moved by 1% of the time
where the time goes in v1:
time: 108 us; the launch traced here: 107 us
  starting transfers between devices  23.3 us (22%)
  local copies, waits for them, and re-layouts  20.3 us (19%)
  waiting for transfers between devices  16 us (15%)
  loops' own time  15.6 us (14%)
  other arithmetic  11.7 us (11%)
  blocking collectives  9.29 us (9%)
  matrix products  9.28 us (9%)
  between operations  1.59 us (1%)
    another operation x1, loops' own time, per_device(): lax.scan(gather_block, start_acc, block_inputs)  11.6 us
    all_to_all x1, blocking collectives, per_device(): lax.all_to_all(reply_rows, 'clump', split_axis=0, concat_axis=0, tiled=True)  9.29 us
    unnamed x34, local copies, waits for them, and re-layouts  7.96 us
    all_to_all x1, starting transfers between devices, per_device(): lax.all_to_all(outgoing[1], 'clump', split_axis=0, concat_axis=0, tiled=T...  7.44 us
    all_to_all x1, waiting for transfers between devices, per_device(): lax.all_to_all(outgoing[0], 'clump', split_axis=0, concat_axis=0, tiled=T...  6.28 us
    all_to_all x1, starting transfers between devices, per_device(): lax.all_to_all(outgoing[0], 'clump', split_axis=0, concat_axis=0, tiled=T...  5.99 us
    all_to_all x1, waiting for transfers between devices, per_device(): lax.all_to_all(lax.all_to_all(reply_rows, 'clump', split_axis=0, concat_a...  4.08 us
    another operation x1, loops' own time, per_device(): lax.map(spread_block, (home_blocks, alive_mask.reshape(blocks, block), sc...  3.99 us
  transfers between devices with their start and end apart: 5, of which 4 were waited for; matrix products, arithmetic and copies ran while one was open for 22% of the time, Pallas kernels for 0%

profile of v1, /device:TPU:0, one launch (start us, length us, event | category | flops | bytes accessed | tf_op | source)
XLA Modules:
  0.0 107.0 jit_solution(13205045787295517161)
XLA Ops:
  2.6 7.4 %all-to-all-start = ((f32[8,4,8]{2,1,0:T(4,128)}), f32[8,4,8]{2,1,0:T(4,128)S(1)}, u32[]{:S(2)}, u32[]{:S(2)}) async-start(f32[8,4,8]{2,1,0:T(4,128)} %reshape.154), calls=%async_computation | async-start | bytes 32768 | tf_op jit(solution)/shard_map/all_to_all | solution.py:119
  10.1 1.5 %convolution_multiply_fusion = f32[1024,64]{0,1:T(8,128)S(1)} fusion(f32[16,64]{1,0:T(8,128)S(1)} %copy-done, f32[1,1024,64]{1,2,0:T(8,128)} %param.17, s32[1024]{0:T(1024)S(1)} %bitcast.160), kind=kOutput, calls=%fused_computation.43 | convolution fusion | flops 12664832 | bytes 532480 | tf_op jit(solution)/shard_map/dot_general | solution.py:46
  17.9 26.8 %while.26 = (s32[]{:T(128)}, f32[640,64]{0,1:T(8,128)S(1)}, f32[640]{0:T(1024)S(1)}, s32[2,512]{1,0:T(2,128)S(1)}, s32[2,512]{1,0:T(2,128)S(1)}, /*index=5*/f32[...) while((s32[]{:T(128)}, f32[640,64]{0,1:T(8,128)S(1)}, ...), condition=%wide.region_3.4_spmd.clone, body=%wide.region_2.3_spmd.clone.sunk | while | flops 218176016 | bytes 1268031 | solution.py:83
  29.7 0.8 dynamic_update_slice.24
  43.0 1.0 dynamic_update_slice.24
  45.0 0.8 reshape.183
  45.7 6.0 %all-to-all-start.2 = ((f32[8,1,2048]{2,1,0:T(1,128)}), f32[8,1,2048]{2,1,0:T(1,128)S(1)}, u32[]{:S(2)}, u32[]{:S(2)}) async-start(f32[8,1,2048]{2,1,0:T(1,128)} %reshape.183), calls=%async_computation.2 | async-start | bytes 131072 | tf_op jit(solution)/shard_map/all_to_all | solution.py:109
  52.4 6.3 %all-to-all-done.2 = f32[8,1,2048]{2,1,0:T(1,128)S(1)} async-done(((f32[8,1,2048]{2,1,0:T(1,128)}), f32[8,1,2048]{2,1,0:T(1,128)S(1)}, u32[]{:S(2)}, u32[]{:S(2)}) %all-to-all-start.2) | async-done | bytes 65568 | tf_op jit(solution)/shard_map/all_to_all | solution.py:109
  58.6 3.3 %all-to-all-start.1 = ((f32[4,8,1,8]{3,1,2,0:T(8,128)}), f32[4,8,1,8]{3,1,2,0:T(8,128)S(1)}, u32[]{:S(2)}, u32[]{:S(2)}) async-start(f32[4,8,1,8]{3,1,2,0:T(8,128)} %pad_maximum_fusion), calls=%async_computation.1 | async-start | bytes 32768 | tf_op jit(solution)/shard_map/all_to_all | solution.py:116
  62.5 0.8 reduce.8
  63.3 0.8 reshape.185
  64.1 1.6 %all-to-all-done.1 = f32[4,8,1,8]{3,1,2,0:T(8,128)S(1)} async-done(((f32[4,8,1,8]{3,1,2,0:T(8,128)}), f32[4,8,1,8]{3,1,2,0:T(8,128)S(1)}, u32[]{:S(2)}, u32[]{:S(2)}) %all-to-all-start.1) | async-done | bytes 1056 | tf_op jit(solution)/shard_map/all_to_all | solution.py:116
  65.7 3.3 %all-to-all-start.3 = ((f32[4,1,4096]{2,1,0:T(1,128)}), f32[4,1,4096]{2,1,0:T(1,128)S(1)}, u32[]{:S(2)}, u32[]{:S(2)}) async-start(f32[4,1,4096]{2,1,0:T(1,128)} %reshape.185), calls=%async_computation.3 | async-start | bytes 131072 | tf_op jit(solution)/shard_map/all_to_all | solution.py:108
  69.1 4.0 %all-to-all-done.3 = f32[4,1,4096]{2,1,0:T(1,128)S(1)} async-done(((f32[4,1,4096]{2,1,0:T(1,128)}), f32[4,1,4096]{2,1,0:T(1,128)S(1)}, u32[]{:S(2)}, u32[]{:S(2)}) %all-to-all-start.3) | async-done | bytes 65568 | tf_op jit(solution)/shard_map/all_to_all | solution.py:108
  73.1 0.8 reduce.9
  75.8 9.3 %all_to_all.30 = f32[8,1,2048]{2,1,0:T(1,128)S(1)} all-to-all(f32[8,1,2048]{2,1,0:T(1,128)S(1)} %reshape.187), channel_id=1, replica_groups=mesh['clump'=8,'grp'=4] {'clump'}, dimensions={0} | all-to-all | bytes 131072 | tf_op jit(solution)/shard_map/all_to_all | solution.py:143
  85.1 0.8 reduce.10
  86.8 3.3 %all-to-all-start.5 = ((f32[4,1,4096]{2,1,0:T(1,128)}), f32[4,1,4096]{2,1,0:T(1,128)S(1)}, u32[]{:S(2)}, u32[]{:S(2)}) async-start(f32[4,1,4096]{2,1,0:T(1,128)} %reshape.189), calls=%async_computation.5 | async-start | bytes 131072 | tf_op jit(solution)/shard_map/all_to_all | solution.py:142
  90.1 4.1 %all-to-all-done.5 = f32[4,1,4096]{2,1,0:T(1,128)S(1)} async-done(((f32[4,1,4096]{2,1,0:T(1,128)}), f32[4,1,4096]{2,1,0:T(1,128)S(1)}, u32[]{:S(2)}, u32[]{:S(2)}) %all-to-all-start.5) | async-done | bytes 65568 | tf_op jit(solution)/shard_map/all_to_all | solution.py:142
  94.1 0.8 reduce.11
  95.3 10.7 %while.25 = (s32[]{:T(128)}, f32[2,512,64]{1,0,2:T(2,128)S(1)}, f32[2,512]{1,0:T(2,128)S(1)}, f32[2,512,64]{1,0,2:T(2,128)S(1)}, s32[2,512]{1,0:T(2,128)S(1)}, /...) while((s32[]{:T(128)}, f32[2,512,64]{1,0,2:T(2,128)S(1)}, f32[2,512]{1,0:T(2,128)S(1)}, ...), condition=%wide.region_5.6_spmd, body=%wide.region_4.5_spmd.sunk | while | flops 201654784 | bytes 1192099 | solution.py:160
  99.5 1.2 %dynamic_update_slice.22 = f32[2,512,64]{1,0,2:T(2,128)S(1)} dynamic-update-slice(f32[2,512,64]{1,0,2:T(2,128)S(1)} %get-tuple-element.390, f32[1,512,64]{1,0,2:T(1,128)S(1)} %copy.70, s32[]{:T(128)} %get-tuple-element.389, s32[]{:T(128)} %constant.46.clone.1..sunk, s32[]{:T(128)} %constant.46.clone.1..sunk) | dynamic-update-slice | bytes 262148 | tf_op jit(solution)/shard_map/while/body/jit(dynamic_update_index_in_dim)/dynamic_update_slice | solution.py:160
  104.8 1.2 %dynamic_update_slice.22 = f32[2,512,64]{1,0,2:T(2,128)S(1)} dynamic-update-slice(f32[2,512,64]{1,0,2:T(2,128)S(1)} %get-tuple-element.390, f32[1,512,64]{1,0,2:T(1,128)S(1)} %copy.70, s32[]{:T(128)} %get-tuple-element.389, s32[]{:T(128)} %constant.46.clone.1..sunk, s32[]{:T(128)} %constant.46.clone.1..sunk) | dynamic-update-slice | bytes 262148 | tf_op jit(solution)/shard_map/while/body/jit(dynamic_update_index_in_dim)/dynamic_update_slice | solution.py:160
  106.1 0.9 reshape.160
  (118 shorter events, 30.1 us)
Async XLA Ops:
  0.6 9.4 %copy-start = (f32[16,64]{1,0:T(8,128)S(1)}, f32[16,64]{1,0:T(8,128)}, u32[]{:S(2)}) copy-start(f32[16,64]{1,0:T(8,128)} %param.27) | copy-start | bytes 12292
  0.6 0.7 copy-start.11
  2.6 7.5 %copy-start.3 = (s32[1,1024]{1,0:T(1,128)S(1)}, s32[1,1024]{1,0:T(1,128)}, u32[]{:S(2)}) copy-start(s32[1,1024]{1,0:T(1,128)} %param.18) | copy-start | bytes 12292
  2.6 43.1 %all-to-all-start = ((f32[8,4,8]{2,1,0:T(4,128)}), f32[8,4,8]{2,1,0:T(4,128)S(1)}, u32[]{:S(2)}, u32[]{:S(2)}) async-start(f32[8,4,8]{2,1,0:T(4,128)} %reshape.154), calls=%async_computation | async-start | bytes 32768 | tf_op jit(solution)/shard_map/all_to_all | solution.py:119
  12.5 0.7 copy-start.6
  13.2 0.7 copy-start.4
  14.5 0.7 copy-start.5
  15.9 0.7 copy-start.8
  16.5 0.7 copy-start.7
  17.2 0.7 copy-start.9
  45.7 12.9 %all-to-all-start.2 = ((f32[8,1,2048]{2,1,0:T(1,128)}), f32[8,1,2048]{2,1,0:T(1,128)S(1)}, u32[]{:S(2)}, u32[]{:S(2)}) async-start(f32[8,1,2048]{2,1,0:T(1,128)} %reshape.183), calls=%async_computation.2 | async-start | bytes 131072 | tf_op jit(solution)/shard_map/all_to_all | solution.py:109
  52.4 9.5 %copy-start.10 = (f32[128]{0:T(128)S(1)}, f32[128]{0:T(128)}, u32[]{:S(2)}) copy-start(f32[128]{0:T(128)} %param.28) | copy-start | bytes 1540
  58.6 7.1 %all-to-all-start.1 = ((f32[4,8,1,8]{3,1,2,0:T(8,128)}), f32[4,8,1,8]{3,1,2,0:T(8,128)S(1)}, u32[]{:S(2)}, u32[]{:S(2)}) async-start(f32[4,8,1,8]{3,1,2,0:T(8,128)} %pad_maximum_fusion), calls=%async_computation.1 | async-start | bytes 32768 | tf_op jit(solution)/shard_map/all_to_all | solution.py:116
  65.7 7.4 %all-to-all-start.3 = ((f32[4,1,4096]{2,1,0:T(1,128)}), f32[4,1,4096]{2,1,0:T(1,128)S(1)}, u32[]{:S(2)}, u32[]{:S(2)}) async-start(f32[4,1,4096]{2,1,0:T(1,128)} %reshape.185), calls=%async_computation.3 | async-start | bytes 131072 | tf_op jit(solution)/shard_map/all_to_all | solution.py:108
  74.0 0.8 copy-start.2
  75.1 0.6 copy-start.1
  86.8 7.4 %all-to-all-start.5 = ((f32[4,1,4096]{2,1,0:T(1,128)}), f32[4,1,4096]{2,1,0:T(1,128)S(1)}, u32[]{:S(2)}, u32[]{:S(2)}) async-start(f32[4,1,4096]{2,1,0:T(1,128)} %reshape.189), calls=%async_computation.5 | async-start | bytes 131072 | tf_op jit(solution)/shard_map/all_to_all | solution.py:142
